TPU v7x, 256 devices: a whole 4x4x8 slice. The times are simulated.
256 devices in a mesh: img: 32 (over y, x, core), strip: 8 (over z).
Axes of the slice: x: 4, y: 4, z: 8, core: 2. Of those that a mesh axis runs over, the one named last changes fastest.
Arguments:
- image_in: bfloat16 [32, 256, 128, 128], P('img', 'strip'), may hold values from -6 to 6
- cotangent: bfloat16 [32, 256, 128, 128], P('img', 'strip'), may hold values from -6 to 6
- conv1_w: bfloat16 [3, 3, 128, 128], replicated, may hold values from -0.1875 to 0.1875
- conv2_w: bfloat16 [3, 3, 128, 128], replicated, may hold values from -0.1875 to 0.1875
- norm1_gain: float32 [128], replicated, may hold values from 0.5 to 1.5
- norm1_shift: float32 [128], replicated, may hold values from -3 to 3
- norm2_gain: float32 [128], replicated, may hold values from 0.5 to 1.5
- norm2_shift: float32 [128], replicated, may hold values from -3 to 3
- strip_rows: int32 [32, 8], P('img', 'strip'), may hold values from 1 to 32, 128 in all within a row
Outputs:
- image_grad: bfloat16 [32, 256, 128, 128], P('img', 'strip')
- conv1_grad: float32 [1152, 128], P('img')
- conv2_grad: float32 [1152, 128], P('img')
- norm_grads: float32 [4, 128], replicated
Inputs may be any that keep to these rules, and one draw needn't show every extreme that they name: `strip_rows`: each image's 8 strip lengths sum to 128; in every image one strip holds exactly 32 rows.
All inputs are finite; a program needn't handle non-finite values. No bound on the sum of `strip_rows` on one device may be relied on, other than what follows from the above.
Results may differ from a plain program's by a relative error of at most 0.0055.
Values may be sent and summed in bfloat16 or wider, within the bound.
No kernel may reach another device: no remote copies, remote signals or barrier semaphores. Data moves between devices by JAX's collectives and lax.ppermute only.
A program may use at most 64 MiB of HBM per device.

v0:
```python
import jax
import jax.numpy as jnp
from jax import lax
from jax.experimental import pallas as pl
from jax.experimental.pallas import tpu as pltpu
from jax.sharding import Mesh
from jax.sharding import PartitionSpec as P


IMG = ("img_0", "img_1", "img_2")
EPSILON = 1e-06
F32 = jnp.float32
BF16 = jnp.bfloat16
SLOTS = 32
COLS = 128
CH = 128
HEIGHT = 128
PER_GROUP = 4
PEERS = 8
CELLS = float(HEIGHT * COLS * PER_GROUP)
WIDE = 3 * CH
PAIR = 2 * WIDE
STEPS = 4
MIB = 1 << 20

VMEM = pl.BlockSpec(memory_space=pltpu.VMEM)
SMEM = pl.BlockSpec(memory_space=pltpu.SMEM)
HBM = pl.BlockSpec(memory_space=pltpu.HBM)


def shape(dims, dtype):
    return jax.ShapeDtypeStruct(dims, dtype)


def call(body, in_specs, outs, flops=0, moved=0, scratch=(), limit=12 * MIB, outs_in=None, aliases=None):
    return pl.pallas_call(
        body,
        in_specs=in_specs,
        out_specs=outs_in or [VMEM] * len(outs),
        out_shape=outs,
        scratch_shapes=scratch,
        input_output_aliases=aliases or {},
        compiler_params=pltpu.CompilerParams(vmem_limit_bytes=limit),
        cost_estimate=pl.CostEstimate(flops=flops, bytes_accessed=moved, transcendentals=0),
    )


def folded(row):
    lanes = jnp.broadcast_to(row, (8, CH))
    lane = lax.broadcasted_iota(jnp.int32, (8, CH), 1)
    lanes = lanes + jnp.where(lane % 2 == 0, pltpu.roll(lanes, CH - 1, 1), pltpu.roll(lanes, 1, 1))
    lanes = lanes + jnp.where(lane % 4 < 2, pltpu.roll(lanes, CH - 2, 1), pltpu.roll(lanes, 2, 1))
    return lanes[0:1]


def group_stats(stats):
    total = stats[0, 0:1]
    for j in range(1, PEERS):
        total = total + stats[j, 0:1]
    mean = folded(total) / CELLS
    spread = jnp.zeros((1, CH), F32)
    for j in range(PEERS):
        count = stats[j, 2:3] * float(COLS)
        gap = stats[j, 0:1] / count - mean
        spread = spread + stats[j, 1:2] + count * gap * gap
    return mean, lax.rsqrt(folded(spread) / CELLS + EPSILON)


def moments(sums, gain):
    cross, plain = sums[0, 0:1], sums[0, 1:2]
    for j in range(1, PEERS):
        cross, plain = cross + sums[j, 0:1], plain + sums[j, 1:2]
    return folded(cross * gain) / CELLS, folded(plain * gain) / CELLS


def sums8(value):
    return jnp.sum(value.reshape(-1, 8, value.shape[-1]), axis=0)


def send(out_ref, rows):
    index = lax.broadcasted_iota(jnp.int32, (8, CH), 0)
    tile = jnp.zeros((8, CH), F32)
    for k, row in enumerate(rows):
        tile = jnp.where(index == k, row, tile)
    for j in range(PEERS):
        out_ref[j] = tile


def kept_sums(value, r, length):
    return jnp.where(r < length, sums8(value), 0.0)


def channel_stats(load, length, out_ref, total=None, more=()):
    if total is None:
        total = sum(kept_sums(load(r), r, length) for r in range(SLOTS))
    total = jnp.sum(total, axis=0, keepdims=True)
    used = length.astype(F32)
    mean = total / (used * float(COLS))
    spread = jnp.zeros((8, CH), F32)
    for r in range(SLOTS):
        gap = load(r) - mean
        spread = spread + kept_sums(gap * gap, r, length)
    send(out_ref, [total, jnp.sum(spread, axis=0, keepdims=True), jnp.broadcast_to(used, (1, CH)), *more])


def sigmoid(z):
    return 0.5 * jnp.tanh(0.5 * z) + 0.5


def taps(row):
    col = lax.broadcasted_iota(jnp.int32, (8, CH), 0)
    before, after = pltpu.roll(row, 1, 0), pltpu.roll(row, COLS - 1, 0)
    before = jnp.concatenate([jnp.where(col == 0, 0.0, before[0:8]), before[8:]], axis=0)
    after = jnp.concatenate([after[:-8], jnp.where(col == 7, 0.0, after[-8:])], axis=0)
    return jnp.concatenate([before.astype(BF16), row.astype(BF16), after.astype(BF16)], axis=1)


def convolve(buf, tile_of, pair_ref, row_at, finish, beside=lambda step: None, chunk=4):
    pair_ref[3 * WIDE :, 0:CH] = jnp.zeros((WIDE, CH), BF16)
    pair_ref[0:WIDE, CH:] = jnp.zeros((WIDE, CH), BF16)
    for tap in range(9):
        tile = tile_of(tap)
        pair_ref[tap * CH : (tap + 1) * CH, 0:CH] = tile
        pair_ref[WIDE + tap * CH : WIDE + (tap + 1) * CH, CH:] = tile
    built = 0
    for begin in range(0, SLOTS // 2, chunk):
        needed = 2 * (begin + chunk) + 2 if row_at else 0
        for t in range(built, needed):
            buf[t // 2, :, t % 2 * WIDE : (t % 2 + 1) * WIDE] = taps(row_at(t))
        built = needed
        beside(begin // chunk)
        upper = buf[begin : begin + chunk].reshape(chunk * COLS, PAIR)
        lower = buf[begin + 1 : begin + 1 + chunk].reshape(chunk * COLS, PAIR)
        out = jnp.dot(
            jnp.concatenate([upper, lower], axis=1), pair_ref[...], preferred_element_type=F32
        )
        out = out.reshape(chunk, COLS, 2 * CH)
        for k in range(chunk):
            finish(2 * (begin + k), out[k, :, 0:CH])
            finish(2 * (begin + k) + 1, out[k, :, CH:])


def ahead(w_ref):
    return lambda tap: w_ref[tap * CH : (tap + 1) * CH]


def turned(w_ref):
    return lambda tap: w_ref[(8 - tap) * CH : (9 - tap) * CH].T


def place_halo(buf, length, above, below):
    buf[0, :, 0:WIDE] = above
    pair = (length + 1) // 2

    @pl.when(length % 2 == 1)
    def _():
        buf[pair, :, 0:WIDE] = below

    @pl.when(length % 2 == 0)
    def _():
        buf[pair, :, WIDE:PAIR] = below


def around(own, up, down, length, t):
    if t == 0:
        return up
    if t == SLOTS + 1:
        return down
    return jnp.where(t <= length, own(t - 1), down)


def in_image(length, strip, t):
    if t == 0:
        return strip > 0
    return (t <= length) | (strip < PEERS - 1)


def transposed_row(tile, i, ahead, keep, out_ref):
    tile = tile.T
    for tap in range(3):
        o = i + ahead - tap
        lanes = (o // 2 + 1) * COLS
        kept = jnp.where(keep(o), tile, jnp.zeros_like(tile))
        out_ref[o % 2, tap * CH : (tap + 1) * CH, lanes : lanes + COLS] = kept


def kernel_grad(rows_t, even, odd):
    used = slice(COLS, COLS + even.shape[0] * COLS)
    grad = jnp.dot(rows_t[0, :, used], even.reshape(-1, WIDE), preferred_element_type=F32)
    return grad + jnp.dot(rows_t[1, :, used], odd.reshape(-1, WIDE), preferred_element_type=F32)


def stats_kernel(
    len_ref, x_ref, g_ref, gain_ref, shift_ref, top_ref, bottom_ref, out_ref,
    rows_ref, gain_own, shift_own, sem, edge_sem, param_sem,
):
    length = len_ref[0, 0]
    last = length - 1
    step = SLOTS // STEPS
    started = []
    for k in range(STEPS):
        part = pl.ds(k * step, step)
        started.append(pltpu.make_async_copy(x_ref.at[part], rows_ref.at[part], sem.at[k]))
    for k, ref in enumerate((x_ref, g_ref)):
        started.append(pltpu.make_async_copy(ref.at[0], top_ref.at[k], edge_sem.at[2 * k]))
        started.append(pltpu.make_async_copy(ref.at[last], bottom_ref.at[k], edge_sem.at[2 * k + 1]))
    for copy in started:
        copy.start()
    params = ((gain_ref, gain_own), (shift_ref, shift_own))
    params = [pltpu.make_async_copy(ref, own, param_sem.at[k]) for k, (ref, own) in enumerate(params)]
    for copy in params:
        copy.start()
    total = jnp.zeros((8, CH), F32)
    for k in range(STEPS):
        started[k].wait()
        for r in range(k * step, (k + 1) * step):
            total = total + kept_sums(rows_ref[r].astype(F32), r, length)
    for copy in params:
        copy.wait()
    more = [gain_own[...], shift_own[...]]
    channel_stats(lambda r: rows_ref[r].astype(F32), length, out_ref, total, more)
    for copy in started[STEPS:]:
        copy.wait()


def act1_of(st_ref):
    mean, inv = group_stats(st_ref)
    scale, shift = inv * st_ref[0, 3:4], st_ref[0, 4:5]

    def act(row):
        pre = (row.astype(F32) - mean) * scale + shift
        return pre * sigmoid(pre)

    return act


def act1_kernel(x_ref, st_ref, act_ref):
    act = act1_of(st_ref)
    act_ref[0, :, 0:WIDE] = jnp.zeros((COLS, WIDE), BF16)
    act_ref[SLOTS // 2, :, WIDE:PAIR] = jnp.zeros((COLS, WIDE), BF16)
    for t in range(1, SLOTS + 1):
        act_ref[t // 2, :, t % 2 * WIDE : (t % 2 + 1) * WIDE] = taps(act(x_ref[t - 1]))


def hidden_kernel(
    len_ref, own_ref, up_ref, down_ref, st_ref, w_ref, hid_ref, act_ref, out_ref, pair_ref
):
    del own_ref
    length, strip = len_ref[0, 0], lax.axis_index("strip")
    act = act1_of(st_ref)
    place_halo(
        act_ref,
        length,
        taps(jnp.where(strip > 0, act(up_ref[0]), 0.0)),
        taps(jnp.where(strip < PEERS - 1, act(down_ref[0]), 0.0)),
    )
    total = [jnp.zeros((8, CH), F32)]

    def finish(r, row):
        hid_ref[r] = row
        total[0] = total[0] + kept_sums(row, r, length)

    convolve(act_ref, ahead(w_ref), pair_ref, None, finish)
    channel_stats(lambda r: hid_ref[r], length, out_ref, total[0])


def back_kernel(len_ref, g_ref, up_ref, down_ref, w_ref, act_ref, g_taps_ref, back_ref, act_t_ref, pair_ref):
    length, strip = len_ref[0, 0], lax.axis_index("strip")

    def row_at(t):
        row = around(lambda r: g_ref[r], up_ref[1], down_ref[1], length, t)
        return jnp.where(in_image(length, strip, t), row.astype(F32), 0.0)

    def finish(r, row):
        back_ref[r] = row

    def beside(step):
        for i in range(step * 9, min(step * 9 + 9, SLOTS + 2)):
            tile = act_ref[i // 2, :, i % 2 * WIDE + CH : i % 2 * WIDE + 2 * CH]
            transposed_row(tile, i, 0, lambda o: (o >= 0) & (o < length), act_t_ref)

    convolve(g_taps_ref, turned(w_ref), pair_ref, row_at, finish, beside)


def dpre2_kernel(
    len_ref, st_ref, hid_ref, back_ref, gain_ref, shift_ref, act_ref, dpre_ref, top_ref, bottom_ref, out_ref
):
    length = len_ref[0, 0]
    mean, inv = group_stats(st_ref)
    gain, shift = gain_ref[...], shift_ref[...]

    cross = plain = jnp.zeros((8, CH), F32)
    for r in range(SLOTS):
        normed = (hid_ref[r] - mean) * inv
        pre = normed * gain + shift
        s = sigmoid(pre)
        act = pre * s
        act_ref[r] = act.astype(BF16)
        grad = jnp.where(r < length, back_ref[r] * (s + act * (1.0 - s)), 0.0)
        dpre_ref[r] = grad
        plain = plain + sums8(grad)
        cross = cross + sums8(grad * normed)
    send(out_ref, [jnp.sum(cross, axis=0, keepdims=True), jnp.sum(plain, axis=0, keepdims=True)])
    for ref, row in ((top_ref, 0), (bottom_ref, length - 1)):
        ref[0] = dpre_ref[row]
        ref[1] = hid_ref[row]


def grad2_kernel(len_ref, act_ref, g_taps_ref, out_ref, act_t_ref):
    length = len_ref[0, 0]
    half = SLOTS // 2
    for tap, o in ((0, 0), (0, 1), (1, 0), (1, SLOTS + 1), (2, SLOTS), (2, SLOTS + 1)):
        lanes = (o // 2 + 1) * COLS
        act_t_ref[o % 2, tap * CH : (tap + 1) * CH, lanes : lanes + COLS] = jnp.zeros((CH, COLS), BF16)
    for i in range(SLOTS):
        transposed_row(act_ref[i], i, 2, lambda o: i < length, act_t_ref)
    out_ref[...] = kernel_grad(
        act_t_ref, g_taps_ref[0 : half + 1, :, 0:WIDE], g_taps_ref[0 : half + 1, :, WIDE:PAIR]
    )


def dpre1_kernel(
    len_ref, st1_ref, st2_ref, sums_ref, own_sums_ref, hid_ref, dpre2_ref, up_ref, down_ref, act_t_ref,
    x_ref, grad2_ref, w_ref, gain1_ref, shift1_ref, gain2_ref,
    share_ref, dpre_ref, out_ref, d_taps_ref, grad1_ref, pair_ref,
):
    length, strip = len_ref[0, 0], lax.axis_index("strip")
    half = SLOTS // 2
    mean2, inv2 = group_stats(st2_ref)
    gain2 = gain2_ref[...]
    cross2, plain2 = moments(sums_ref, gain2)

    by_dpre, by_hidden, level = inv2 * gain2, inv2 * inv2 * cross2, inv2 * plain2

    def dhidden(dpre, hidden):
        return dpre * by_dpre - (hidden - mean2) * by_hidden - level

    mean1, inv1 = group_stats(st1_ref)
    gain1, shift1 = gain1_ref[...], shift1_ref[...]
    sums = [jnp.zeros((8, CH), F32), jnp.zeros((8, CH), F32)]

    def row_at(t):
        dpre = around(lambda r: dpre2_ref[r], up_ref[0], down_ref[0], length, t)
        hidden = around(lambda r: hid_ref[r], up_ref[1], down_ref[1], length, t)
        return jnp.where(in_image(length, strip, t), dhidden(dpre, hidden), 0.0)

    def finish(r, row):
        normed = (x_ref[r].astype(F32) - mean1) * inv1
        pre = normed * gain1 + shift1
        s = sigmoid(pre)
        grad = jnp.where(r < length, row * (s + pre * s * (1.0 - s)), 0.0)
        dpre_ref[r] = grad
        sums[0] = sums[0] + sums8(grad * normed)
        sums[1] = sums[1] + sums8(grad)

    convolve(d_taps_ref, turned(w_ref), pair_ref, row_at, finish, chunk=1)
    grad1_ref[...] = kernel_grad(act_t_ref, d_taps_ref[0:half, :, WIDE:PAIR], d_taps_ref[1 : half + 1, :, 0:WIDE])
    cross, plain = (jnp.sum(total, axis=0, keepdims=True) for total in sums)
    index = lax.broadcasted_iota(jnp.int32, (8, CH), 0)
    norm = jnp.where(index == 0, cross, jnp.where(index == 1, plain, 0.0))
    out_ref[...] = norm
    norm = norm + jnp.where(index == 2, own_sums_ref[0, 0:1], 0.0) + jnp.where(index == 3, own_sums_ref[0, 1:2], 0.0)
    blocks, rows = share_ref.shape[0], (share_ref.shape[1] - 8) // 2
    for j in range(blocks):
        share_ref[j] = packed(cut(grad1_ref, j * rows, rows), cut(grad2_ref, j * rows, rows), norm)


def cut(ref, begin, count):
    pieces = []
    while count:
        tap, row = divmod(begin, CH)
        here = min(count, CH - row)
        a, b = divmod(tap, 3)
        pieces.append(ref[a * CH + row : a * CH + row + here, (2 - b) * CH : (3 - b) * CH])
        begin, count = begin + here, count - here
    return pieces


def packed(first, second, norm):
    high = norm.astype(BF16).astype(F32)
    return jnp.concatenate([*first, *second, high[0:4], (norm - high)[0:4]], axis=0).astype(BF16)


def unpacked(total):
    rows = (total.shape[0] - 8) // 2
    norm = total[2 * rows : 2 * rows + 4] + total[2 * rows + 4 :]
    return total[0:rows], total[rows : 2 * rows], norm


def relay_kernel(in_ref, own_ref, out_ref):
    total = in_ref[0].astype(F32)
    for j in range(1, in_ref.shape[0]):
        total = total + in_ref[j].astype(F32)
    first, second, norm = unpacked(total)
    norm = jnp.concatenate([norm, jnp.zeros((4, CH), F32)], axis=0)
    own = own_ref[...]
    high = own.astype(BF16).astype(F32)
    image = jnp.concatenate([high[0:4], (own - high)[0:4]], axis=0).astype(BF16)
    tile = jnp.concatenate([packed([first], [second], norm), image], axis=0)
    for j in range(PEERS):
        out_ref[j] = tile


def finish_kernel(
    len_ref, in_ref, st_ref, x_ref, g_ref, dpre_ref, gain_ref, image_ref, first_ref, second_ref, norm_ref,
    rows_ref, first_own, second_own, norm_own, sem,
):
    total = in_ref[0].astype(F32)
    for j in range(1, PEERS):
        total = total + in_ref[j].astype(F32)
    rows = first_ref.shape[0]
    first_own[...], second_own[...], norm_own[...] = unpacked(total[0 : 2 * rows + 8])
    copies = []
    for k, (own, ref) in enumerate(((first_own, first_ref), (second_own, second_ref), (norm_own, norm_ref))):
        copies.append(pltpu.make_async_copy(own, ref, sem.at[STEPS + k]))
        copies[k].start()
    sums = total[2 * rows + 8 : 2 * rows + 12] + total[2 * rows + 12 : 2 * rows + 16]
    length = len_ref[0, 0]
    mean, inv = group_stats(st_ref)
    gain = gain_ref[...]
    cross, plain = folded(sums[0:1] * gain) / CELLS, folded(sums[1:2] * gain) / CELLS
    by_dpre, by_x, level = inv * gain, inv * inv * cross, inv * plain
    step = SLOTS // STEPS
    for k in range(STEPS):
        for r in range(k * step, (k + 1) * step):
            grad = dpre_ref[r] * by_dpre - (x_ref[r].astype(F32) - mean) * by_x - level
            rows_ref[r] = jnp.where(r < length, g_ref[r].astype(F32) + grad, 0.0).astype(BF16)
        part = pl.ds(k * step, step)
        copies.append(pltpu.make_async_copy(rows_ref.at[part], image_ref.at[part], sem.at[k]))
        copies[-1].start()
    for copy in copies:
        copy.wait()


def exchanged(value, axis):
    return lax.all_to_all(value, axis, split_axis=0, concat_axis=0, tiled=True)


def shifted(value, by):
    return lax.ppermute(value, "strip", [(i, (i + by) % PEERS) for i in range(PEERS)])


def body(
    image_in, cotangent, conv1_w, conv2_w, norm1_gain, norm1_shift, norm2_gain, norm2_shift, strip_rows
):
    x, g = image_in[0], cotangent[0]
    gain1, shift1 = norm1_gain[None], norm1_shift[None]
    gain2, shift2 = norm2_gain[None], norm2_shift[None]
    images = lax.axis_size(IMG)
    half = SLOTS // 2
    field = SLOTS * COLS * CH
    conv_flops = 2 * 9 * field * CH
    edge = (COLS, CH)
    stat = shape((PEERS, 8, CH), F32)

    ahead1, ahead2 = conv1_w.reshape(9 * CH, CH), conv2_w.reshape(9 * CH, CH)
    pair = pltpu.VMEM((2 * PAIR, 2 * CH), BF16)
    top, bottom, stats1 = call(
        stats_kernel,
        [SMEM] + [HBM] * 4,
        [shape((2, *edge), BF16), shape((2, *edge), BF16), stat],
        flops=field * 6,
        moved=field * 2,
        scratch=[
            pltpu.VMEM((SLOTS, *edge), BF16), pltpu.VMEM((1, CH), F32), pltpu.VMEM((1, CH), F32),
            pltpu.SemaphoreType.DMA((STEPS,)), pltpu.SemaphoreType.DMA((4,)), pltpu.SemaphoreType.DMA((2,)),
        ],
        limit=63 * MIB + MIB // 4,
    )(strip_rows, x, g, gain1, shift1)
    up, down = shifted(bottom, 1), shifted(top, -1)
    stats1 = exchanged(stats1, "strip")

    (act1,) = call(
        act1_kernel, [VMEM] * 2, [shape((half + 1, COLS, PAIR), BF16)], flops=field * 20, moved=field * 4
    )(x, stats1)
    hidden, act1, stats2 = call(
        hidden_kernel,
        [SMEM] + [VMEM] * 5,
        [shape((SLOTS, *edge), F32), shape((half + 1, COLS, PAIR), BF16), stat],
        flops=conv_flops,
        moved=field * 6,
        scratch=[pair],
        aliases={1: 1},
    )(strip_rows, act1, up, down, stats1, ahead1)

    g_taps, back2, act1_t = call(
        back_kernel,
        [SMEM] + [VMEM] * 5,
        [
            shape((half + 1, COLS, PAIR), BF16),
            shape((SLOTS, *edge), F32),
            shape((2, WIDE, (half + 2) * COLS), BF16),
        ],
        flops=conv_flops,
        moved=field * 6,
        scratch=[pair],
    )(strip_rows, g, up, down, ahead2, act1)
    stats2, g_taps, back2, act1_t = lax.optimization_barrier((stats2, g_taps, back2, act1_t))
    stats2 = exchanged(stats2, "strip")

    act2, dpre2, top, bottom, own_sums2 = call(
        dpre2_kernel,
        [SMEM] + [VMEM] * 5,
        [
            shape((SLOTS, *edge), BF16), shape((SLOTS, *edge), F32), shape((2, *edge), F32), shape((2, *edge), F32), stat,
        ],
        flops=field * 40,
        moved=field * 8,
    )(strip_rows, stats2, hidden, back2, gain2, shift2)
    up, down = shifted(bottom, 1), shifted(top, -1)

    (grad2,) = call(
        grad2_kernel,
        [SMEM] + [VMEM] * 2,
        [shape((WIDE, WIDE), F32)],
        flops=conv_flops,
        moved=field * 6,
        scratch=[pltpu.VMEM((2, WIDE, (half + 2) * COLS), BF16)],
    )(strip_rows, act2, g_taps)
    own_sums2, grad2 = lax.optimization_barrier((own_sums2, grad2))
    sums2 = exchanged(own_sums2, "strip")

    rows = 9 * CH // images
    share, dpre1, own_sums1 = call(
        dpre1_kernel,
        [SMEM] + [VMEM] * 15,
        [shape((images, 2 * rows + 8, CH), BF16), shape((SLOTS, *edge), F32), shape((8, CH), F32)],
        flops=2 * conv_flops,
        moved=field * 8,
        scratch=[pltpu.VMEM((half + 1, COLS, PAIR), BF16), pltpu.VMEM((WIDE, WIDE), F32), pair],
    )(
        strip_rows, stats1, stats2, sums2, own_sums2, hidden, dpre2, up, down, act1_t, x, grad2, ahead1,
        gain1, shift1, gain2,
    )
    share, dpre1, own_sums1 = lax.optimization_barrier((share, dpre1, own_sums1))
    share = exchanged(share, IMG)
    (relayed,) = call(
        relay_kernel, [VMEM, VMEM], [shape((PEERS, 2 * rows + 16, CH), BF16)], moved=images * (2 * rows + 8) * CH * 2
    )(share, own_sums1)
    relayed = exchanged(relayed, "strip")
    image_grad, grad1, grad2, norm_grads = call(
        finish_kernel,
        [SMEM] + [VMEM] * 6,
        [shape((SLOTS, *edge), BF16), shape((rows, CH), F32), shape((rows, CH), F32), shape((4, CH), F32)],
        flops=field * 12,
        moved=field * 10,
        scratch=[
            pltpu.VMEM((SLOTS, *edge), BF16), pltpu.VMEM((rows, CH), F32), pltpu.VMEM((rows, CH), F32),
            pltpu.VMEM((4, CH), F32), pltpu.SemaphoreType.DMA((STEPS + 3,)),
        ],
        outs_in=[HBM] * 4,
    )(strip_rows, relayed, stats1, x, g, dpre1, gain1)
    return image_grad[None], grad1, grad2, norm_grads


def solution(mesh):
    torus = Mesh(mesh.devices.reshape(4, 4, 2, mesh.shape["strip"]), (*IMG, "strip"))
    return jax.shard_map(
        body,
        mesh=torus,
        in_specs=(
            P(IMG, "strip", None, None), P(IMG, "strip", None, None), P(), P(), P(), P(), P(), P(), P(IMG, "strip"),
        ),
        out_specs=(P(IMG, "strip", None, None), P(IMG, None), P(IMG, None), P()),
        check_vma=False,
    )
```

profile of v0, /device:TPU:1, one launch (start us, length us, event | category | flops | bytes accessed | tf_op | source)
XLA Modules:
  0.0 98.5 jit_solution(10558478523806874265)
XLA Ops:
  0.6 0.0 copy-start.4
  1.3 2.3 %shard_map.120 = (bf16[2,128,128]{2,1,0:T(8,128)(2,1)}, bf16[2,128,128]{2,1,0:T(8,128)(2,1)}, f32[8,8,128]{2,1,0:T(8,128)}) custom-call(s32[1,1]{1,0:T(1,128)S(6)} %copy.15.len_ref, bf16[32,128,128]{2,1,0:T(8,128)(2,1)} %bitcast.9, bf16[32,128,128]{2,1,0:T(8,128)(2,1)} %bitcast.13, f32[1,128]{1,0:T(1,128)} %bitcast.19, f32[1,128]{1,0:T(1,128)} %bitcast.22), custom_call_target="tpu_custom_call" | custom-call | flops 3145728 | bytes 1048576 | tf_op jit(solution)/shard_map/pallas_call | solution.py:458
  3.7 2.5 %collective-permute-start = (bf16[2,128,128]{2,1,0:T(8,128)(2,1)}, bf16[2,128,128]{2,1,0:T(8,128)(2,1)S(1)}, u32[]{:S(2)}, u32[]{:S(2)}) collective-permute-start(bf16[2,128,128]{2,1,0:T(8,128)(2,1)} %get-tuple-element.32), channel_id=1, source_target_pairs={{0,1},{1,2},{2,3},{3,4},{4,5},{5,6},{6,7},{7,0},{8,9},{9,10},{10,1... | collective-permute-start | bytes 196616 | tf_op jit(solution)/shard_map/ppermute | solution.py:440
  6.2 4.0 %collective-permute-start.1 = (bf16[2,128,128]{2,1,0:T(8,128)(2,1)}, bf16[2,128,128]{2,1,0:T(8,128)(2,1)S(1)}, u32[]{:S(2)}, u32[]{:S(2)}) collective-permute-start(bf16[2,128,128]{2,1,0:T(8,128)(2,1)} %get-tuple-element.33), channel_id=1, source_target_pairs={{0,7},{1,0},{2,1},{3,2},{4,3},{5,4},{6,5},{7,6},{8,15},{9,8},{10,9... | collective-permute-start | bytes 196616 | tf_op jit(solution)/shard_map/ppermute | solution.py:440
  10.2 12.1 %all_to_all.25.st_ref.st1_ref = f32[8,8,128]{2,1,0:T(8,128)S(1)} all-to-all(f32[8,8,128]{2,1,0:T(8,128)} %get-tuple-element.31), channel_id=1, replica_groups=mesh['img_0'=4,'img_1'=4,'img_2'=2,'strip'=8] {'strip'}, dimensions={0} | all-to-all | bytes 65536 | tf_op jit(solution)/shard_map/all_to_all | solution.py:436
  22.4 0.0 copy-start
  22.4 1.2 %copy-done = bf16[1,32,128,128]{3,2,1,0:T(8,128)(2,1)S(1)} copy-done((bf16[1,32,128,128]{3,2,1,0:T(8,128)(2,1)S(1)}, bf16[1,32,128,128]{3,2,1,0:T(8,128)(2,1)}, u32[]{:S(2)}) %copy-start) | copy-done | bytes 1048600
  23.6 1.4 %shard_map.121.own_ref = bf16[17,128,768]{2,1,0:T(8,128)(2,1)S(1)} custom-call(bf16[32,128,128]{2,1,0:T(8,128)(2,1)S(1)} %bitcast.10, f32[8,8,128]{2,1,0:T(8,128)S(1)} %all_to_all.25.st_ref.st1_ref), custom_call_target="tpu_custom_call" | custom-call | flops 10485760 | bytes 2097152 | tf_op jit(solution)/shard_map/pallas_call | solution.py:473
  24.9 0.0 copy-start.2
  25.0 0.0 copy-start.3
  25.0 0.0 collective-permute-done.up_ref
  25.0 0.0 collective-permute-done.1.down_ref
  25.0 0.0 copy-done.4
  25.0 2.5 %shard_map.122 = (f32[32,128,128]{2,1,0:T(8,128)S(1)}, bf16[17,128,768]{2,1,0:T(8,128)(2,1)S(1)}, f32[8,8,128]{2,1,0:T(8,128)S(1)}) custom-call(s32[1,1]{1,0:T(1,128)S(6)} %copy.15.len_ref, bf16[17,128,768]{2,1,0:T(8,128)(2,1)S(1)} %shard_map.121.own_ref, bf16[2,128,128]{2,1,0:T(8,128)(2,1)S(1)} %collective-permute-done.up_ref, ...), custom_call_target="tpu_custom_call", output_to_operand_aliasing={{1}: (1, {})} | custom-call | flops 1207959552 | bytes 3145728 | tf_op jit(solution)/shard_map/pallas_call | solution.py:476
  27.5 0.0 copy-start.7
  27.5 0.0 copy-start.8
  27.5 0.0 copy-done.2
  27.5 0.0 copy-done.3
  27.5 2.3 %shard_map.123 = (bf16[17,128,768]{2,1,0:T(8,128)(2,1)S(1)}, f32[32,128,128]{2,1,0:T(8,128)S(1)}, bf16[2,384,2304]{2,1,0:T(8,128)(2,1)S(1)}) custom-call(s32[1,1]{1,0:T(1,128)S(6)} %copy.15.len_ref, bf16[32,128,128]{2,1,0:T(8,128)(2,1)S(1)} %bitcast.14, bf16[2,128,128]{2,1,0:T(8,128)(2,1)S(1)} %collective-permute-done.up_ref, ...), custom_call_target="tpu_custom_call" | custom-call | flops 1207959552 | bytes 3145728 | tf_op jit(solution)/shard_map/pallas_call | solution.py:486
  29.8 9.2 %all_to_all.26.st_ref.st2_ref = f32[8,8,128]{2,1,0:T(8,128)S(1)} all-to-all(f32[8,8,128]{2,1,0:T(8,128)S(1)} %get-tuple-element.39), channel_id=1, replica_groups=mesh['img_0'=4,'img_1'=4,'img_2'=2,'strip'=8] {'strip'}, dimensions={0} | all-to-all | bytes 65536 | tf_op jit(solution)/shard_map/all_to_all | solution.py:436
  39.0 0.0 copy-done.7
  39.0 0.0 copy-done.8
  39.0 1.6 %shard_map.124 = (bf16[32,128,128]{2,1,0:T(8,128)(2,1)S(1)}, f32[32,128,128]{2,1,0:T(8,128)S(1)}, f32[2,128,128]{2,1,0:T(8,128)S(1)}, f32[2,128,128]{2,1,0:T(8,128)S(1)}, f32[8,8,128]{2,1,0:T(8,128)S(1)}) custom-call(s32[1,1]{1,0:T(1,128)S(6)} %copy.15.len_ref, f32[8,8,128]{2,1,0:T(8,128)S(1)} %all_to_all.26.st_ref.st2_ref, ...), custom_call_target="tpu_custom_call" | custom-call | flops 20971520 | bytes 4194304 | tf_op jit(solution)/shard_map/pallas_call | solution.py:501
  40.6 0.0 copy-start.1
  40.7 0.0 copy-start.5
  40.7 0.0 copy-start.6
  40.7 0.4 collective-permute-start.2
  41.0 2.4 %collective-permute-start.3 = (f32[2,128,128]{2,1,0:T(8,128)S(1)}, f32[2,128,128]{2,1,0:T(8,128)S(1)}, u32[]{:S(2)}, u32[]{:S(2)}) collective-permute-start(f32[2,128,128]{2,1,0:T(8,128)S(1)} %get-tuple-element.48), channel_id=1, source_target_pairs={{0,7},{1,0},{2,1},{3,2},{4,3},{5,4},{6,5},{7,6},{8,15},{9,8},{10,9... | collective-permute-start | bytes 393224 | tf_op jit(solution)/shard_map/ppermute | solution.py:440
  43.4 2.0 %shard_map.125.grad2_ref = f32[384,384]{1,0:T(8,128)S(1)} custom-call(s32[1,1]{1,0:T(1,128)S(6)} %copy.15.len_ref, bf16[32,128,128]{2,1,0:T(8,128)(2,1)S(1)} %get-tuple-element.43.act_ref, bf16[17,128,768]{2,1,0:T(8,128)(2,1)S(1)} %get-tuple-element.44.g_taps_ref), custom_call_target="tpu_custom_call" | custom-call | flops 1207959552 | bytes 3145728 | tf_op jit(solution)/shard_map/pallas_call | solution.py:512
  45.4 9.2 %all_to_all.27.sums_ref = f32[8,8,128]{2,1,0:T(8,128)S(1)} all-to-all(f32[8,8,128]{2,1,0:T(8,128)S(1)} %get-tuple-element.45.own_sums_ref), channel_id=1, replica_groups=mesh['img_0'=4,'img_1'=4,'img_2'=2,'strip'=8] {'strip'}, dimensions={0} | all-to-all | bytes 65536 | tf_op jit(solution)/shard_map/all_to_all | solution.py:436
  54.7 0.0 collective-permute-done.2.up_ref
  54.7 0.0 collective-permute-done.3.down_ref
  54.7 0.0 copy-done.1
  54.7 0.0 copy-done.5
  54.7 0.0 copy-done.6
  54.7 5.0 %shard_map.126 = (bf16[32,80,128]{2,1,0:T(8,128)(2,1)S(1)}, f32[32,128,128]{2,1,0:T(8,128)S(1)}, f32[8,128]{1,0:T(8,128)S(1)}) custom-call(s32[1,1]{1,0:T(1,128)S(6)} %copy.15.len_ref, f32[8,8,128]{2,1,0:T(8,128)S(1)} %all_to_all.25.st_ref.st1_ref, f32[8,8,128]{2,1,0:T(8,128)S(1)} %all_to_all.26.st_ref.st2_ref, f32[8,8,128]{2,1,0:T(8,128)S(1)} %all_to_all.27.sums_ref, ...), custom_call_target="tpu_custom_call" | custom-call | flops 2415919104 | bytes 4194304 | tf_op jit(solution)/shard_map/pallas_call | solution.py:524
  59.7 25.2 %all_to_all.28.in_ref = bf16[32,80,128]{2,1,0:T(8,128)(2,1)S(1)} all-to-all(bf16[32,80,128]{2,1,0:T(8,128)(2,1)S(1)} %get-tuple-element.51), channel_id=1, replica_groups=mesh['img_0'=4,'img_1'=4,'img_2'=2,'strip'=8] {'img_0','img_1','img_2'}, dimensions={0} | all-to-all | bytes 1310720 | tf_op jit(solution)/shard_map/all_to_all | solution.py:436
  84.9 0.1 shard_map.127
  85.0 11.7 %all_to_all.29.in_ref = bf16[8,88,128]{2,1,0:T(8,128)(2,1)S(1)} all-to-all(bf16[8,88,128]{2,1,0:T(8,128)(2,1)S(1)} %shard_map.127), channel_id=1, replica_groups=mesh['img_0'=4,'img_1'=4,'img_2'=2,'strip'=8] {'strip'}, dimensions={0} | all-to-all | bytes 360448 | tf_op jit(solution)/shard_map/all_to_all | solution.py:436
  96.7 1.7 %shard_map.128 = (bf16[32,128,128]{2,1,0:T(8,128)(2,1)}, f32[36,128]{1,0:T(8,128)}, f32[36,128]{1,0:T(8,128)}, f32[4,128]{1,0:T(4,128)}) custom-call(s32[1,1]{1,0:T(1,128)S(6)} %copy.15.len_ref, bf16[8,88,128]{2,1,0:T(8,128)(2,1)S(1)} %all_to_all.29.in_ref, f32[8,8,128]{2,1,0:T(8,128)S(1)} %all_to_all.25.st_ref.st1_ref, bf16[32,128,128]{2,1,0:T(8,128)(2,1)S(1)} %bitcast.12, ...), custom_call_target="tpu_custom_call" | custom-call | flops 6291456 | bytes 5242880 | tf_op jit(solution)/shard_map/pallas_call | solution.py:541
Async XLA Ops:
  0.6 24.4 %copy-start.4 = (bf16[3,3,128,128]{3,2,1,0:T(8,128)(2,1)S(1)}, bf16[3,3,128,128]{3,2,1,0:T(8,128)(2,1)}, u32[]{:S(2)}) copy-start(bf16[3,3,128,128]{3,2,1,0:T(8,128)(2,1)} %param.11) | copy-start | bytes 884740
  3.7 21.3 %collective-permute-start = (bf16[2,128,128]{2,1,0:T(8,128)(2,1)}, bf16[2,128,128]{2,1,0:T(8,128)(2,1)S(1)}, u32[]{:S(2)}, u32[]{:S(2)}) collective-permute-start(bf16[2,128,128]{2,1,0:T(8,128)(2,1)} %get-tuple-element.32), channel_id=1, source_target_pairs={{0,1},{1,2},{2,3},{3,4},{4,5},{5,6},{6,7},{7,0},{8,9},{9,10},{10,1... | collective-permute-start | bytes 196616 | tf_op jit(solution)/shard_map/ppermute | solution.py:440
  6.2 18.8 %collective-permute-start.1 = (bf16[2,128,128]{2,1,0:T(8,128)(2,1)}, bf16[2,128,128]{2,1,0:T(8,128)(2,1)S(1)}, u32[]{:S(2)}, u32[]{:S(2)}) collective-permute-start(bf16[2,128,128]{2,1,0:T(8,128)(2,1)} %get-tuple-element.33), channel_id=1, source_target_pairs={{0,7},{1,0},{2,1},{3,2},{4,3},{5,4},{6,5},{7,6},{8,15},{9,8},{10,9... | collective-permute-start | bytes 196616 | tf_op jit(solution)/shard_map/ppermute | solution.py:440
  22.4 1.2 %copy-start = (bf16[1,32,128,128]{3,2,1,0:T(8,128)(2,1)S(1)}, bf16[1,32,128,128]{3,2,1,0:T(8,128)(2,1)}, u32[]{:S(2)}) copy-start(bf16[1,32,128,128]{3,2,1,0:T(8,128)(2,1)} %param.9) | copy-start | bytes 3145732
  24.9 2.6 %copy-start.2 = (bf16[1,32,128,128]{3,2,1,0:T(8,128)(2,1)S(1)}, bf16[1,32,128,128]{3,2,1,0:T(8,128)(2,1)}, u32[]{:S(2)}) copy-start(bf16[1,32,128,128]{3,2,1,0:T(8,128)(2,1)} %param.10) | copy-start | bytes 3145732
  25.0 2.6 %copy-start.3 = (bf16[3,3,128,128]{3,2,1,0:T(8,128)(2,1)S(1)}, bf16[3,3,128,128]{3,2,1,0:T(8,128)(2,1)}, u32[]{:S(2)}) copy-start(bf16[3,3,128,128]{3,2,1,0:T(8,128)(2,1)} %param.12) | copy-start | bytes 884740
  27.5 11.6 %copy-start.7 = (f32[128]{0:T(128)S(1)}, f32[128]{0:T(128)}, u32[]{:S(2)}) copy-start(f32[128]{0:T(128)} %param.15) | copy-start | bytes 1540
  27.5 11.5 %copy-start.8 = (f32[128]{0:T(128)S(1)}, f32[128]{0:T(128)}, u32[]{:S(2)}) copy-start(f32[128]{0:T(128)} %param.16) | copy-start | bytes 1540
  40.6 14.0 %copy-start.1 = (bf16[1,32,128,128]{3,2,1,0:T(8,128)(2,1)S(1)}, bf16[1,32,128,128]{3,2,1,0:T(8,128)(2,1)}, u32[]{:S(2)}) copy-start(bf16[1,32,128,128]{3,2,1,0:T(8,128)(2,1)} %param.9) | copy-start | bytes 3145732
  40.7 14.0 %copy-start.5 = (f32[128]{0:T(128)S(1)}, f32[128]{0:T(128)}, u32[]{:S(2)}) copy-start(f32[128]{0:T(128)} %param.13) | copy-start | bytes 1540
  40.7 14.0 %copy-start.6 = (f32[128]{0:T(128)S(1)}, f32[128]{0:T(128)}, u32[]{:S(2)}) copy-start(f32[128]{0:T(128)} %param.14) | copy-start | bytes 1540
  40.7 14.0 %collective-permute-start.2 = (f32[2,128,128]{2,1,0:T(8,128)S(1)}, f32[2,128,128]{2,1,0:T(8,128)S(1)}, u32[]{:S(2)}, u32[]{:S(2)}) collective-permute-start(f32[2,128,128]{2,1,0:T(8,128)S(1)} %get-tuple-element.47), channel_id=1, source_target_pairs={{0,1},{1,2},{2,3},{3,4},{4,5},{5,6},{6,7},{7,0},{8,9},{9,10},{10,1... | collective-permute-start | bytes 393224 | tf_op jit(solution)/shard_map/ppermute | solution.py:440
  41.0 13.6 %collective-permute-start.3 = (f32[2,128,128]{2,1,0:T(8,128)S(1)}, f32[2,128,128]{2,1,0:T(8,128)S(1)}, u32[]{:S(2)}, u32[]{:S(2)}) collective-permute-start(f32[2,128,128]{2,1,0:T(8,128)S(1)} %get-tuple-element.48), channel_id=1, source_target_pairs={{0,7},{1,0},{2,1},{3,2},{4,3},{5,4},{6,5},{7,6},{8,15},{9,8},{10,9... | collective-permute-start | bytes 393224 | tf_op jit(solution)/shard_map/ppermute | solution.py:440
where the time goes:
time: 98.9 us; the launch traced here: 98.5 us
  blocking collectives  67.5 us (68%)
  Pallas kernels  18.8 us (19%)
  starting transfers between devices  9.31 us (9%)
  between operations  1.66 us (2%)
  local copies, waits for them, and re-layouts  1.27 us (1%)
    all_to_all x5, blocking collectives, exchanged(): return lax.all_to_all(value, axis, split_axis=0, concat_axis=0, tiled=True)  67.5 us
    ppermute x4, starting transfers between devices, shifted(): lax.ppermute(value, 'strip', [(i, (i + by) % PEERS) for i in range(PEERS)])  9.31 us
    pallas_call x1, Pallas kernels, body(): call(dpre1_kernel, [SMEM] + [VMEM] * 15, [shape((images, 2 * rows + 8, CH...  4.98 us
    pallas_call x1, Pallas kernels, body(): call(hidden_kernel, [SMEM] + [VMEM] * 5, [shape((SLOTS, *edge), F32), sha...  2.49 us
    pallas_call x1, Pallas kernels, body(): call(stats_kernel, [SMEM] + [HBM] * 4, [shape((2, *edge), BF16), shape((2...  2.35 us
    pallas_call x1, Pallas kernels, body(): call(back_kernel, [SMEM] + [VMEM] * 5, [shape((half + 1, COLS, PAIR), BF1...  2.25 us
    pallas_call x1, Pallas kernels, body(): call(grad2_kernel, [SMEM] + [VMEM] * 2, [shape((WIDE, WIDE), F32)], flops...  1.98 us
  transfers between devices with their start and end apart: 4, of which 0 were waited for; matrix products, arithmetic and copies ran while one was open for 0% of the time, Pallas kernels for 3%

commit v1 on v0

--- a/solution.py
+++ b/solution.py
@@ -103,8 +103,10 @@
     send(out_ref, [total, jnp.sum(spread, axis=0, keepdims=True), jnp.broadcast_to(used, (1, CH)), *more])
 
 
-def sigmoid(z):
-    return 0.5 * jnp.tanh(0.5 * z) + 0.5
+def silu_parts(half):
+    t = jnp.tanh(half)
+    act = half * (1.0 + t)
+    return act, 0.5 * ((1.0 + t) + act * (1.0 - t))
 
 
 def taps(row):
@@ -225,11 +227,10 @@
 
 def act1_of(st_ref):
     mean, inv = group_stats(st_ref)
-    scale, shift = inv * st_ref[0, 3:4], st_ref[0, 4:5]
+    scale, shift = 0.5 * (inv * st_ref[0, 3:4]), 0.5 * st_ref[0, 4:5]
 
     def act(row):
-        pre = (row.astype(F32) - mean) * scale + shift
-        return pre * sigmoid(pre)
+        return silu_parts((row.astype(F32) - mean) * scale + shift)[0]
 
     return act
 
@@ -287,16 +288,14 @@
 ):
     length = len_ref[0, 0]
     mean, inv = group_stats(st_ref)
-    gain, shift = gain_ref[...], shift_ref[...]
+    gain, shift = 0.5 * gain_ref[...], 0.5 * shift_ref[...]
 
     cross = plain = jnp.zeros((8, CH), F32)
     for r in range(SLOTS):
         normed = (hid_ref[r] - mean) * inv
-        pre = normed * gain + shift
-        s = sigmoid(pre)
-        act = pre * s
+        act, slope = silu_parts(normed * gain + shift)
         act_ref[r] = act.astype(BF16)
-        grad = jnp.where(r < length, back_ref[r] * (s + act * (1.0 - s)), 0.0)
+        grad = jnp.where(r < length, back_ref[r] * slope, 0.0)
         dpre_ref[r] = grad
         plain = plain + sums8(grad)
         cross = cross + sums8(grad * normed)
@@ -336,7 +335,7 @@
         return dpre * by_dpre - (hidden - mean2) * by_hidden - level
 
     mean1, inv1 = group_stats(st1_ref)
-    gain1, shift1 = gain1_ref[...], shift1_ref[...]
+    gain1, shift1 = 0.5 * gain1_ref[...], 0.5 * shift1_ref[...]
     sums = [jnp.zeros((8, CH), F32), jnp.zeros((8, CH), F32)]
 
     def row_at(t):
@@ -346,9 +345,8 @@
 
     def finish(r, row):
         normed = (x_ref[r].astype(F32) - mean1) * inv1
-        pre = normed * gain1 + shift1
-        s = sigmoid(pre)
-        grad = jnp.where(r < length, row * (s + pre * s * (1.0 - s)), 0.0)
+        _, slope = silu_parts(normed * gain1 + shift1)
+        grad = jnp.where(r < length, row * slope, 0.0)
         dpre_ref[r] = grad
         sums[0] = sums[0] + sums8(grad * normed)
         sums[1] = sums[1] + sums8(grad)

time: 98.9 us -> 98.7 us (level)
  no operation moved by 1% of the time
where the time goes in v1:
time: 98.7 us; the launch traced here: 98.3 us
  blocking collectives  67.5 us (68%)
  Pallas kernels  18.5 us (19%)
  starting transfers between devices  9.31 us (9%)
  between operations  1.65 us (2%)
  local copies, waits for them, and re-layouts  1.27 us (1%)
    all_to_all x5, blocking collectives, exchanged(): return lax.all_to_all(value, axis, split_axis=0, concat_axis=0, tiled=True)  67.5 us
    ppermute x4, starting transfers between devices, shifted(): lax.ppermute(value, 'strip', [(i, (i + by) % PEERS) for i in range(PEERS)])  9.31 us
    pallas_call x1, Pallas kernels, body(): call(dpre1_kernel, [SMEM] + [VMEM] * 15, [shape((images, 2 * rows + 8, CH...  4.91 us
    pallas_call x1, Pallas kernels, body(): call(hidden_kernel, [SMEM] + [VMEM] * 5, [shape((SLOTS, *edge), F32), sha...  2.48 us
    pallas_call x1, Pallas kernels, body(): call(stats_kernel, [SMEM] + [HBM] * 4, [shape((2, *edge), BF16), shape((2...  2.35 us
    pallas_call x1, Pallas kernels, body(): call(back_kernel, [SMEM] + [VMEM] * 5, [shape((half + 1, COLS, PAIR), BF1...  2.25 us
    pallas_call x1, Pallas kernels, body(): call(grad2_kernel, [SMEM] + [VMEM] * 2, [shape((WIDE, WIDE), F32)], flops...  1.98 us
  transfers between devices with their start and end apart: 4, of which 0 were waited for; matrix products, arithmetic and copies ran while one was open for 0% of the time, Pallas kernels for 3%

profile of v1, /device:TPU:1, one launch (start us, length us, event | category | flops | bytes accessed | tf_op | source)
XLA Modules:
  0.0 98.3 jit_solution(8768164820152074636)
XLA Ops:
  0.6 0.0 copy-start.4
  1.3 2.3 %shard_map.120 = (bf16[2,128,128]{2,1,0:T(8,128)(2,1)}, bf16[2,128,128]{2,1,0:T(8,128)(2,1)}, f32[8,8,128]{2,1,0:T(8,128)}) custom-call(s32[1,1]{1,0:T(1,128)S(6)} %copy.15.len_ref, bf16[32,128,128]{2,1,0:T(8,128)(2,1)} %bitcast.9, bf16[32,128,128]{2,1,0:T(8,128)(2,1)} %bitcast.13, f32[1,128]{1,0:T(1,128)} %bitcast.19, f32[1,128]{1,0:T(1,128)} %bitcast.22), custom_call_target="tpu_custom_call" | custom-call | flops 3145728 | bytes 1048576 | tf_op jit(solution)/shard_map/pallas_call | solution.py:456
  3.7 2.5 %collective-permute-start = (bf16[2,128,128]{2,1,0:T(8,128)(2,1)}, bf16[2,128,128]{2,1,0:T(8,128)(2,1)S(1)}, u32[]{:S(2)}, u32[]{:S(2)}) collective-permute-start(bf16[2,128,128]{2,1,0:T(8,128)(2,1)} %get-tuple-element.32), channel_id=1, source_target_pairs={{0,1},{1,2},{2,3},{3,4},{4,5},{5,6},{6,7},{7,0},{8,9},{9,10},{10,1... | collective-permute-start | bytes 196616 | tf_op jit(solution)/shard_map/ppermute | solution.py:438
  6.2 4.0 %collective-permute-start.1 = (bf16[2,128,128]{2,1,0:T(8,128)(2,1)}, bf16[2,128,128]{2,1,0:T(8,128)(2,1)S(1)}, u32[]{:S(2)}, u32[]{:S(2)}) collective-permute-start(bf16[2,128,128]{2,1,0:T(8,128)(2,1)} %get-tuple-element.33), channel_id=1, source_target_pairs={{0,7},{1,0},{2,1},{3,2},{4,3},{5,4},{6,5},{7,6},{8,15},{9,8},{10,9... | collective-permute-start | bytes 196616 | tf_op jit(solution)/shard_map/ppermute | solution.py:438
  10.2 12.1 %all_to_all.25.st_ref.st1_ref = f32[8,8,128]{2,1,0:T(8,128)S(1)} all-to-all(f32[8,8,128]{2,1,0:T(8,128)} %get-tuple-element.31), channel_id=1, replica_groups=mesh['img_0'=4,'img_1'=4,'img_2'=2,'strip'=8] {'strip'}, dimensions={0} | all-to-all | bytes 65536 | tf_op jit(solution)/shard_map/all_to_all | solution.py:434
  22.4 0.0 copy-start
  22.4 1.2 %copy-done = bf16[1,32,128,128]{3,2,1,0:T(8,128)(2,1)S(1)} copy-done((bf16[1,32,128,128]{3,2,1,0:T(8,128)(2,1)S(1)}, bf16[1,32,128,128]{3,2,1,0:T(8,128)(2,1)}, u32[]{:S(2)}) %copy-start) | copy-done | bytes 1048600
  23.6 1.2 %shard_map.121.own_ref = bf16[17,128,768]{2,1,0:T(8,128)(2,1)S(1)} custom-call(bf16[32,128,128]{2,1,0:T(8,128)(2,1)S(1)} %bitcast.10, f32[8,8,128]{2,1,0:T(8,128)S(1)} %all_to_all.25.st_ref.st1_ref), custom_call_target="tpu_custom_call" | custom-call | flops 10485760 | bytes 2097152 | tf_op jit(solution)/shard_map/pallas_call | solution.py:471
  24.8 0.0 copy-start.2
  24.8 0.0 copy-start.3
  24.8 0.0 collective-permute-done.up_ref
  24.8 0.0 collective-permute-done.1.down_ref
  24.9 0.0 copy-done.4
  24.9 2.5 %shard_map.122 = (f32[32,128,128]{2,1,0:T(8,128)S(1)}, bf16[17,128,768]{2,1,0:T(8,128)(2,1)S(1)}, f32[8,8,128]{2,1,0:T(8,128)S(1)}) custom-call(s32[1,1]{1,0:T(1,128)S(6)} %copy.15.len_ref, bf16[17,128,768]{2,1,0:T(8,128)(2,1)S(1)} %shard_map.121.own_ref, bf16[2,128,128]{2,1,0:T(8,128)(2,1)S(1)} %collective-permute-done.up_ref, ...), custom_call_target="tpu_custom_call", output_to_operand_aliasing={{1}: (1, {})} | custom-call | flops 1207959552 | bytes 3145728 | tf_op jit(solution)/shard_map/pallas_call | solution.py:474
  27.3 0.0 copy-start.7
  27.4 0.0 copy-start.8
  27.4 0.0 copy-done.2
  27.4 0.0 copy-done.3
  27.4 2.3 %shard_map.123 = (bf16[17,128,768]{2,1,0:T(8,128)(2,1)S(1)}, f32[32,128,128]{2,1,0:T(8,128)S(1)}, bf16[2,384,2304]{2,1,0:T(8,128)(2,1)S(1)}) custom-call(s32[1,1]{1,0:T(1,128)S(6)} %copy.15.len_ref, bf16[32,128,128]{2,1,0:T(8,128)(2,1)S(1)} %bitcast.14, bf16[2,128,128]{2,1,0:T(8,128)(2,1)S(1)} %collective-permute-done.up_ref, ...), custom_call_target="tpu_custom_call" | custom-call | flops 1207959552 | bytes 3145728 | tf_op jit(solution)/shard_map/pallas_call | solution.py:484
  29.7 9.2 %all_to_all.26.st_ref.st2_ref = f32[8,8,128]{2,1,0:T(8,128)S(1)} all-to-all(f32[8,8,128]{2,1,0:T(8,128)S(1)} %get-tuple-element.39), channel_id=1, replica_groups=mesh['img_0'=4,'img_1'=4,'img_2'=2,'strip'=8] {'strip'}, dimensions={0} | all-to-all | bytes 65536 | tf_op jit(solution)/shard_map/all_to_all | solution.py:434
  38.9 0.0 copy-done.7
  38.9 0.0 copy-done.8
  38.9 1.6 %shard_map.124 = (bf16[32,128,128]{2,1,0:T(8,128)(2,1)S(1)}, f32[32,128,128]{2,1,0:T(8,128)S(1)}, f32[2,128,128]{2,1,0:T(8,128)S(1)}, f32[2,128,128]{2,1,0:T(8,128)S(1)}, f32[8,8,128]{2,1,0:T(8,128)S(1)}) custom-call(s32[1,1]{1,0:T(1,128)S(6)} %copy.15.len_ref, f32[8,8,128]{2,1,0:T(8,128)S(1)} %all_to_all.26.st_ref.st2_ref, ...), custom_call_target="tpu_custom_call" | custom-call | flops 20971520 | bytes 4194304 | tf_op jit(solution)/shard_map/pallas_call | solution.py:499
  40.5 0.0 copy-start.1
  40.5 0.0 copy-start.5
  40.5 0.0 copy-start.6
  40.5 0.4 collective-permute-start.2
  40.9 2.4 %collective-permute-start.3 = (f32[2,128,128]{2,1,0:T(8,128)S(1)}, f32[2,128,128]{2,1,0:T(8,128)S(1)}, u32[]{:S(2)}, u32[]{:S(2)}) collective-permute-start(f32[2,128,128]{2,1,0:T(8,128)S(1)} %get-tuple-element.48), channel_id=1, source_target_pairs={{0,7},{1,0},{2,1},{3,2},{4,3},{5,4},{6,5},{7,6},{8,15},{9,8},{10,9... | collective-permute-start | bytes 393224 | tf_op jit(solution)/shard_map/ppermute | solution.py:438
  43.3 2.0 %shard_map.125.grad2_ref = f32[384,384]{1,0:T(8,128)S(1)} custom-call(s32[1,1]{1,0:T(1,128)S(6)} %copy.15.len_ref, bf16[32,128,128]{2,1,0:T(8,128)(2,1)S(1)} %get-tuple-element.43.act_ref, bf16[17,128,768]{2,1,0:T(8,128)(2,1)S(1)} %get-tuple-element.44.g_taps_ref), custom_call_target="tpu_custom_call" | custom-call | flops 1207959552 | bytes 3145728 | tf_op jit(solution)/shard_map/pallas_call | solution.py:510
  45.2 9.2 %all_to_all.27.sums_ref = f32[8,8,128]{2,1,0:T(8,128)S(1)} all-to-all(f32[8,8,128]{2,1,0:T(8,128)S(1)} %get-tuple-element.45.own_sums_ref), channel_id=1, replica_groups=mesh['img_0'=4,'img_1'=4,'img_2'=2,'strip'=8] {'strip'}, dimensions={0} | all-to-all | bytes 65536 | tf_op jit(solution)/shard_map/all_to_all | solution.py:434
  54.5 0.0 collective-permute-done.2.up_ref
  54.5 0.0 collective-permute-done.3.down_ref
  54.5 0.0 copy-done.1
  54.5 0.0 copy-done.5
  54.5 0.0 copy-done.6
  54.5 4.9 %shard_map.126 = (bf16[32,80,128]{2,1,0:T(8,128)(2,1)S(1)}, f32[32,128,128]{2,1,0:T(8,128)S(1)}, f32[8,128]{1,0:T(8,128)S(1)}) custom-call(s32[1,1]{1,0:T(1,128)S(6)} %copy.15.len_ref, f32[8,8,128]{2,1,0:T(8,128)S(1)} %all_to_all.25.st_ref.st1_ref, f32[8,8,128]{2,1,0:T(8,128)S(1)} %all_to_all.26.st_ref.st2_ref, f32[8,8,128]{2,1,0:T(8,128)S(1)} %all_to_all.27.sums_ref, ...), custom_call_target="tpu_custom_call" | custom-call | flops 2415919104 | bytes 4194304 | tf_op jit(solution)/shard_map/pallas_call | solution.py:522
  59.4 25.2 %all_to_all.28.in_ref = bf16[32,80,128]{2,1,0:T(8,128)(2,1)S(1)} all-to-all(bf16[32,80,128]{2,1,0:T(8,128)(2,1)S(1)} %get-tuple-element.51), channel_id=1, replica_groups=mesh['img_0'=4,'img_1'=4,'img_2'=2,'strip'=8] {'img_0','img_1','img_2'}, dimensions={0} | all-to-all | bytes 1310720 | tf_op jit(solution)/shard_map/all_to_all | solution.py:434
  84.7 0.1 shard_map.127
  84.8 11.7 %all_to_all.29.in_ref = bf16[8,88,128]{2,1,0:T(8,128)(2,1)S(1)} all-to-all(bf16[8,88,128]{2,1,0:T(8,128)(2,1)S(1)} %shard_map.127), channel_id=1, replica_groups=mesh['img_0'=4,'img_1'=4,'img_2'=2,'strip'=8] {'strip'}, dimensions={0} | all-to-all | bytes 360448 | tf_op jit(solution)/shard_map/all_to_all | solution.py:434
  96.4 1.7 %shard_map.128 = (bf16[32,128,128]{2,1,0:T(8,128)(2,1)}, f32[36,128]{1,0:T(8,128)}, f32[36,128]{1,0:T(8,128)}, f32[4,128]{1,0:T(4,128)}) custom-call(s32[1,1]{1,0:T(1,128)S(6)} %copy.15.len_ref, bf16[8,88,128]{2,1,0:T(8,128)(2,1)S(1)} %all_to_all.29.in_ref, f32[8,8,128]{2,1,0:T(8,128)S(1)} %all_to_all.25.st_ref.st1_ref, bf16[32,128,128]{2,1,0:T(8,128)(2,1)S(1)} %bitcast.12, ...), custom_call_target="tpu_custom_call" | custom-call | flops 6291456 | bytes 5242880 | tf_op jit(solution)/shard_map/pallas_call | solution.py:539
Async XLA Ops:
  0.6 24.2 %copy-start.4 = (bf16[3,3,128,128]{3,2,1,0:T(8,128)(2,1)S(1)}, bf16[3,3,128,128]{3,2,1,0:T(8,128)(2,1)}, u32[]{:S(2)}) copy-start(bf16[3,3,128,128]{3,2,1,0:T(8,128)(2,1)} %param.11) | copy-start | bytes 884740
  3.7 21.2 %collective-permute-start = (bf16[2,128,128]{2,1,0:T(8,128)(2,1)}, bf16[2,128,128]{2,1,0:T(8,128)(2,1)S(1)}, u32[]{:S(2)}, u32[]{:S(2)}) collective-permute-start(bf16[2,128,128]{2,1,0:T(8,128)(2,1)} %get-tuple-element.32), channel_id=1, source_target_pairs={{0,1},{1,2},{2,3},{3,4},{4,5},{5,6},{6,7},{7,0},{8,9},{9,10},{10,1... | collective-permute-start | bytes 196616 | tf_op jit(solution)/shard_map/ppermute | solution.py:438
  6.2 18.6 %collective-permute-start.1 = (bf16[2,128,128]{2,1,0:T(8,128)(2,1)}, bf16[2,128,128]{2,1,0:T(8,128)(2,1)S(1)}, u32[]{:S(2)}, u32[]{:S(2)}) collective-permute-start(bf16[2,128,128]{2,1,0:T(8,128)(2,1)} %get-tuple-element.33), channel_id=1, source_target_pairs={{0,7},{1,0},{2,1},{3,2},{4,3},{5,4},{6,5},{7,6},{8,15},{9,8},{10,9... | collective-permute-start | bytes 196616 | tf_op jit(solution)/shard_map/ppermute | solution.py:438
  22.4 1.2 %copy-start = (bf16[1,32,128,128]{3,2,1,0:T(8,128)(2,1)S(1)}, bf16[1,32,128,128]{3,2,1,0:T(8,128)(2,1)}, u32[]{:S(2)}) copy-start(bf16[1,32,128,128]{3,2,1,0:T(8,128)(2,1)} %param.9) | copy-start | bytes 3145732
  24.8 2.6 %copy-start.2 = (bf16[1,32,128,128]{3,2,1,0:T(8,128)(2,1)S(1)}, bf16[1,32,128,128]{3,2,1,0:T(8,128)(2,1)}, u32[]{:S(2)}) copy-start(bf16[1,32,128,128]{3,2,1,0:T(8,128)(2,1)} %param.10) | copy-start | bytes 3145732
  24.8 2.6 %copy-start.3 = (bf16[3,3,128,128]{3,2,1,0:T(8,128)(2,1)S(1)}, bf16[3,3,128,128]{3,2,1,0:T(8,128)(2,1)}, u32[]{:S(2)}) copy-start(bf16[3,3,128,128]{3,2,1,0:T(8,128)(2,1)} %param.12) | copy-start | bytes 884740
  27.3 11.6 %copy-start.7 = (f32[128]{0:T(128)S(1)}, f32[128]{0:T(128)}, u32[]{:S(2)}) copy-start(f32[128]{0:T(128)} %param.15) | copy-start | bytes 1540
  27.4 11.5 %copy-start.8 = (f32[128]{0:T(128)S(1)}, f32[128]{0:T(128)}, u32[]{:S(2)}) copy-start(f32[128]{0:T(128)} %param.16) | copy-start | bytes 1540
  40.5 14.0 %copy-start.1 = (bf16[1,32,128,128]{3,2,1,0:T(8,128)(2,1)S(1)}, bf16[1,32,128,128]{3,2,1,0:T(8,128)(2,1)}, u32[]{:S(2)}) copy-start(bf16[1,32,128,128]{3,2,1,0:T(8,128)(2,1)} %param.9) | copy-start | bytes 3145732
  40.5 14.0 %copy-start.5 = (f32[128]{0:T(128)S(1)}, f32[128]{0:T(128)}, u32[]{:S(2)}) copy-start(f32[128]{0:T(128)} %param.13) | copy-start | bytes 1540
  40.5 14.0 %copy-start.6 = (f32[128]{0:T(128)S(1)}, f32[128]{0:T(128)}, u32[]{:S(2)}) copy-start(f32[128]{0:T(128)} %param.14) | copy-start | bytes 1540
  40.5 14.0 %collective-permute-start.2 = (f32[2,128,128]{2,1,0:T(8,128)S(1)}, f32[2,128,128]{2,1,0:T(8,128)S(1)}, u32[]{:S(2)}, u32[]{:S(2)}) collective-permute-start(f32[2,128,128]{2,1,0:T(8,128)S(1)} %get-tuple-element.47), channel_id=1, source_target_pairs={{0,1},{1,2},{2,3},{3,4},{4,5},{5,6},{6,7},{7,0},{8,9},{9,10},{10,1... | collective-permute-start | bytes 393224 | tf_op jit(solution)/shard_map/ppermute | solution.py:438
  40.9 13.6 %collective-permute-start.3 = (f32[2,128,128]{2,1,0:T(8,128)S(1)}, f32[2,128,128]{2,1,0:T(8,128)S(1)}, u32[]{:S(2)}, u32[]{:S(2)}) collective-permute-start(f32[2,128,128]{2,1,0:T(8,128)S(1)} %get-tuple-element.48), channel_id=1, source_target_pairs={{0,7},{1,0},{2,1},{3,2},{4,3},{5,4},{6,5},{7,6},{8,15},{9,8},{10,9... | collective-permute-start | bytes 393224 | tf_op jit(solution)/shard_map/ppermute | solution.py:438
